TPU v7x, 32 devices: a whole 2x2x4 slice. The times are simulated.
32 devices in a mesh: section: 8 (over y, x, core), tensor: 4 (over z).
Axes of the slice: x: 2, y: 2, z: 4, core: 2. Of those that a mesh axis runs over, the one named last changes fastest.
Arguments:
- arriving: bfloat16 [8, 512, 16384], P('section', 'tensor'), may hold values from -6 to 6
- kept_input: bfloat16 [8, 512, 16384], P('section', 'tensor'), may hold values from -6 to 6
- returning: bfloat16 [8, 512, 16384], P('section', 'tensor'), may hold values from -6 to 6
- norm_gain: bfloat16 [8, 16384], P('section'), may hold values from 0.25 to 1.75
- key_weight: bfloat16 [8, 16384, 1024], P('section', 'tensor'), may hold values from -0.0625 to 0.0625
- value_weight: bfloat16 [8, 16384, 1024], P('section', 'tensor'), may hold values from -0.0625 to 0.0625
- key_down: bfloat16 [8, 16384, 16], P('section', 'tensor'), may hold values from -0.046875 to 0.046875
- value_down: bfloat16 [8, 16384, 16], P('section', 'tensor'), may hold values from -0.046875 to 0.046875
- key_up: bfloat16 [8, 16, 1024], P('section', None, 'tensor'), may hold values from -1.5 to 1.5
- value_up: bfloat16 [8, 16, 1024], P('section', None, 'tensor'), may hold values from -1.5 to 1.5
- key_cot: bfloat16 [8, 512, 1024], P('section', None, 'tensor'), may hold values from -6 to 6
- value_cot: bfloat16 [8, 512, 1024], P('section', None, 'tensor'), may hold values from -6 to 6
Outputs:
- keys: bfloat16 [8, 512, 1024], P('section', None, 'tensor')
- values: bfloat16 [8, 512, 1024], P('section', None, 'tensor')
- input_grad: bfloat16 [8, 512, 16384], P('section', 'tensor')
- key_down_grad: float32 [8, 16384, 16], P('section', 'tensor')
- value_down_grad: float32 [8, 16384, 16], P('section', 'tensor')
- key_up_grad: float32 [8, 16, 1024], P('section', None, 'tensor')
- value_up_grad: float32 [8, 16, 1024], P('section', None, 'tensor')
All inputs are finite; a program needn't handle non-finite values.
Results may differ from a plain program's by a relative error of at most 0.014.
Values may be sent and summed in bfloat16 or wider, within the bound.
A program may use at most 192 MiB of HBM per device.

v0:
```python
import functools

import jax
import jax.numpy as jnp
from jax import lax
from jax.experimental import pallas as pl
from jax.experimental.pallas import tpu as pltpu
from jax.sharding import PartitionSpec as P

epsilon = 1e-05
adapter_scale = 2.0
bf16 = jnp.bfloat16
f32 = jnp.float32
MESH = pl.DeviceIdType.MESH
lanes = 128
parts = 4
halves = 2
row_tile = 16


def flip(z, mask):
    bit = 1
    while bit <= mask:
        if mask & bit:
            z = z + bit - 2 * bit * ((z // bit) % 2)
        bit *= 2
    return z


def bits_up(count):
    bits = []
    bit = 1
    while bit < count:
        bits.append(bit)
        bit *= 2
    return bits


def dot_nt(a, b):
    return lax.dot_general(a, b, (((1,), (1,)), ((), ())), preferred_element_type=f32)


def dot_nn(a, b):
    return jnp.dot(a, b, preferred_element_type=f32)


def layer_kernel(
    count,
    sections,
    gain_ref,
    arr,
    kept,
    ret,
    wk,
    wv,
    dnk,
    dnv,
    upk,
    upv,
    ck,
    cv,
    keys_out,
    values_out,
    grad_out,
    dgk_out,
    dgv_out,
    ugk_out,
    ugv_out,
    wk_v,
    wv_v,
    cotk,
    cotv,
    upk_v,
    upv_v,
    dn_v,
    arr_v,
    kept_v,
    back_v,
    x_v,
    inv_t,
    inv_in,
    inv_f,
    inv_b,
    ad_v,
    adt_v,
    mid_v,
    bo_v,
    bi_v,
    nb_v,
    dp_v,
    dp_in,
    km_v,
    sums_v,
    sums_in,
    kv_v,
    dg_v,
    ug_v,
    send_sem,
    recv_sem,
    local_sem,
):
    rows, width = kept.shape
    depth = wk.shape[0]
    tokens, heads = ck.shape
    rank = upk.shape[0]
    s = lax.axis_index("section")
    z = lax.axis_index("tensor")
    ahead = lax.rem(s + 1, sections)
    behind = lax.rem(s + sections - 1, sections)
    used = [0, 0]

    def load(src, dst):
        copy = pltpu.make_async_copy(src, dst, local_sem.at[used[1]])
        used[1] += 1
        copy.start()
        return copy

    sent = []

    def send(src, dst, section, tensor):
        k = used[0]
        used[0] += 1
        copy = pltpu.make_async_remote_copy(
            src_ref=src,
            dst_ref=dst,
            send_sem=send_sem.at[k],
            recv_sem=recv_sem.at[k],
            device_id=(section, tensor),
            device_id_type=MESH,
        )
        copy.start()
        sent.append(copy)
        return copy

    def head_cols(q):
        return pl.ds(pl.multiple_of(q * heads, heads), heads)

    def depth_cols(q):
        return pl.ds(pl.multiple_of(q * depth, depth), depth)

    bits = bits_up(count)
    down_bits = list(reversed(bits))
    own = [
        load(ck, cotk.at[:, head_cols(z)]),
        load(cv, cotv.at[:, head_cols(z)]),
        load(upk, upk_v.at[:, head_cols(z)]),
        load(upv, upv_v.at[:, head_cols(z)]),
    ]
    own_down = [load(dnk, dn_v.at[z, :rank]), load(dnv, dn_v.at[z, rank:])]
    arr_load = load(arr, arr_v)
    kept_load = load(kept, kept_v)
    weights = [load(wk, wk_v), load(wv, wv_v)]

    def gather_stage(held, bit, kinds):
        to = flip(z, bit)
        copies = []
        for h in held:
            q = flip(z, h)
            if "c" in kinds:
                for src, dst in ((ck, cotk), (cv, cotv), (upk, upk_v), (upv, upv_v)):
                    block = dst.at[:, head_cols(q)]
                    copies.append(send(block if h else src, block, s, to))
            if "d" in kinds:
                copies.append(send(dn_v.at[q], dn_v.at[q], s, to))
        return copies

    half = rows // halves

    def send_arriving(j, i):
        q = flip(z, j)
        at = pl.ds(i * half, half)
        return send(arr.at[at, depth_cols(q)], x_v.at[z, at], ahead, q)

    far = [j for j in range(count) if j >= max(bits[-1], 1)] if bits else []
    near = [j for j in range(1, count) if j not in far]
    arrivals = {}
    held = [0]
    stage = gather_stage(held, down_bits[0], "c") if bits else []
    for i in range(halves):
        arrivals[0, i] = send_arriving(0, i)
    for j in far:
        arrivals[j, 0] = send_arriving(j, 0)
    returned = send(ret, back_v, behind, z)
    for copy in own_down:
        copy.wait()
    down_stage = gather_stage(held, down_bits[0], "d") if bits else []

    arr_load.wait()

    def arr_stats(i, _):
        at = pl.ds(pl.multiple_of(i * row_tile, row_tile), row_tile)
        x = arr_v[at, :].astype(f32)
        inverse = lax.rsqrt(jnp.mean(x * x, axis=-1, keepdims=True) + epsilon)
        inv_t[at, :] = jnp.broadcast_to(inverse, (row_tile, lanes))
        return 0

    lax.fori_loop(0, rows // row_tile, arr_stats, 0)
    inv_in[z] = inv_t[...].T[:8]
    inverses = [send(inv_in.at[z], inv_in.at[z + count], ahead, flip(z, j)) for j in range(count)]
    kept_load.wait()

    def kept_stats(i, _):
        at = pl.ds(pl.multiple_of(i * row_tile, row_tile), row_tile)
        x = kept_v[at, :].astype(f32)
        inverse = lax.rsqrt(jnp.mean(x * x, axis=-1, keepdims=True) + epsilon)
        inv_b[at, :] = jnp.broadcast_to(inverse, (row_tile, lanes))
        return 0

    lax.fori_loop(0, rows // row_tile, kept_stats, 0)

    for bit in down_bits[:1]:
        for copy in stage:
            copy.wait_recv()
        held = held + [h ^ bit for h in held]
    waiting = list(down_stage)
    for bit in down_bits[1:]:
        stage = gather_stage(held, bit, "c")
        if bit == down_bits[1]:
            for i in range(1, halves):
                for j in far:
                    arrivals[j, i] = send_arriving(j, i)
        for copy in waiting:
            copy.wait_recv()
        waiting = gather_stage(held, bit, "d")
        for copy in stage:
            copy.wait_recv()
        held = held + [h ^ bit for h in held]
    for i in range(halves):
        for j in near + far:
            if (j, i) not in arrivals:
                arrivals[j, i] = send_arriving(j, i)
    for copy in own + weights:
        copy.wait()

    for r, (cot, up) in enumerate(((cotk, upk_v), (cotv, upv_v))):
        ad_v[:, r * rank : (r + 1) * rank] = adapter_scale * dot_nt(cot[...], up[...])
        adt_v[r * rank : (r + 1) * rank, :] = adapter_scale * dot_nt(up[...], cot[...])

    tile = min(512, depth)

    def branch_tile(i, _):
        at = pl.ds(pl.multiple_of(i * tile, tile), tile)
        total = dot_nn(ad_v[...].astype(bf16), dn_v[z, :, at])
        total = total + dot_nt(cotk[...], wk_v[at, :])
        total = total + dot_nt(cotv[...], wv_v[at, :])
        bo_v[:, :, at] = total.astype(bf16).reshape(count, rows, tile)
        return 0

    lax.fori_loop(0, depth // tile, branch_tile, 0)
    part = rows // parts
    others = far + near
    branches = {}

    def send_branch(i):
        at = pl.ds(i * part, part)
        for j in others:
            q = flip(z, j)
            branches[j, i] = send(bo_v.at[q, at], bi_v.at[z, at], s, q)

    for i in range(parts // 2):
        send_branch(i)

    def own_branch(i, _):
        at = pl.ds(pl.multiple_of(i * row_tile, row_tile), row_tile)
        bi_v[z, at, :] = bo_v[z, at, :]
        return 0

    lax.fori_loop(0, rows // row_tile, own_branch, 0)

    for copy in waiting:
        copy.wait_recv()
    mine = adt_v[:, pl.ds(pl.multiple_of(z * rows, rows), rows)].astype(bf16)

    km_v[z] = jnp.zeros((2 * rank, rows), f32)

    def kept_block(j, _):
        inverse = inv_b[:, :1]

        def normalize(i, _):
            at = pl.ds(pl.multiple_of(i * tile, tile), tile)
            cols = pl.ds(pl.multiple_of(j * depth + i * tile, tile), tile)
            part = kept_v[:, cols].astype(f32) * inverse * gain_ref[:, cols].astype(f32)
            nb_v[:, at] = part.astype(bf16)
            return 0

        lax.fori_loop(0, depth // tile, normalize, 0)
        km_v[z] += dot_nt(dn_v[j], nb_v[...])
        dp_v[j] = dot_nn(mine, nb_v[...]).astype(bf16)
        return 0

    lax.fori_loop(0, count, kept_block, 0)
    mids = [send(km_v.at[z], km_v.at[z], s, flip(z, j)) for j in range(1, count)]

    def scatter_stage(buf, landing, bit):
        to = flip(z, bit)
        offset = sum(count // (2 * b) for b in bits if b < bit)
        return [
            send(buf.at[flip(z, bit ^ m)], landing.at[offset + k], s, to)
            for k, m in enumerate(range(0, count, 2 * bit))
        ]

    def scatter_add(buf, landing, bit, copies):
        offset = sum(count // (2 * b) for b in bits if b < bit)
        for k, m in enumerate(range(0, count, 2 * bit)):
            copies[k].wait_recv()
            q = flip(z, m)
            buf[q] = (buf[q].astype(f32) + landing[offset + k].astype(f32)).astype(bf16)

    stores = []
    down_stage = scatter_stage(dp_v, dp_in, bits[0]) if bits else []

    def head_block(q):
        gain_cols = depth_cols(z)

        def scale(i, _):
            at = pl.ds(pl.multiple_of(i * row_tile, row_tile), row_tile)
            x_v[q, at, :] = (x_v[q, at, :].astype(f32) * gain_ref[:, gain_cols].astype(f32)).astype(bf16)
            return 0

        lax.fori_loop(0, rows // row_tile, scale, 0)
        mid = adapter_scale * dot_nt(x_v[q], dn_v[z])
        mid_v[...] = mid.astype(bf16)
        at = pl.ds(pl.multiple_of(q * rows, rows), rows)

        def head_cut(d, _):
            cols = head_cols(d)
            for r, (w, up) in enumerate(((wk_v, upk_v), (wv_v, upv_v))):
                total = dot_nn(x_v[q], w[:, cols])
                total = total + dot_nn(mid_v[:, r * rank : (r + 1) * rank], up[:, cols])
                sums_v[d, r, at, :] = total.astype(bf16)
            return 0

        lax.fori_loop(0, count, head_cut, 0)

    for j in [0] + far + near:
        for i in range(halves):
            arrivals[j, i].wait_recv()
        head_block(flip(z, j))
    for k, bit in enumerate(bits):
        stage = scatter_stage(sums_v, sums_in, bit)
        if k == 0:
            send_branch(parts // 2)
        scatter_add(dp_v, dp_in, bit, down_stage)
        if k + 1 < len(bits):
            down_stage = scatter_stage(dp_v, dp_in, bits[k + 1])
        if k + 1 < len(bits):
            scatter_add(sums_v, sums_in, bit, stage)
    for i in range(parts // 2 + 1, parts):
        send_branch(i)

    dg_v[...] = dp_v[z].astype(f32)
    stores.append(load(dg_v.at[:rank], dgk_out))
    stores.append(load(dg_v.at[rank:], dgv_out))
    for copy in mids:
        copy.wait_recv()
    for r, cot in enumerate((cotk, cotv)):
        total = jnp.zeros((rank, heads), f32)
        for q in range(count):
            mid = (adapter_scale * km_v[q, r * rank : (r + 1) * rank, :]).astype(bf16)
            total = total + dot_nn(mid, cot[q * rows : (q + 1) * rows, head_cols(z)])
        ug_v[r] = total
    stores.append(load(ug_v.at[0], ugk_out))
    stores.append(load(ug_v.at[1], ugv_out))
    for copy in inverses:
        copy.wait_recv()
    for q in range(count):
        spread = jnp.broadcast_to(inv_in[count + q, :1, :], (lanes, rows)).T
        inv_f[q * rows : (q + 1) * rows, :] = spread
    returned.wait_recv()

    def grad_tile(i, _):
        at = pl.ds(pl.multiple_of(i * row_tile, row_tile), row_tile)
        inverse = inv_b[at, :1]
        inner = jnp.zeros((row_tile, 1), f32)
        for j in range(count):
            cols = slice(j * depth, (j + 1) * depth)
            scaled = gain_ref[:, cols].astype(f32) * bi_v[j, at, :].astype(f32)
            inner = inner + jnp.sum(kept_v[at, cols].astype(f32) * scaled, axis=-1, keepdims=True)
        pull = inverse * inverse * inverse * (inner / width)
        for j in range(count):
            cols = slice(j * depth, (j + 1) * depth)
            scaled = gain_ref[:, cols].astype(f32) * bi_v[j, at, :].astype(f32)
            value = back_v[at, cols].astype(f32) + inverse * scaled - kept_v[at, cols].astype(f32) * pull
            arr_v[at, cols] = value.astype(bf16)
        return 0

    def finish(i):
        for j in others:
            branches[j, i].wait_recv()
        lax.fori_loop(i * part // row_tile, (i + 1) * part // row_tile, grad_tile, 0)
        at = pl.ds(i * part, part)
        stores.append(load(arr_v.at[at], grad_out.at[at]))

    for i in range(parts - 1):
        finish(i)

    if bits:
        stage[0].wait_recv()

    def head_tile(i, _):
        at = pl.ds(pl.multiple_of(i * row_tile, row_tile), row_tile)
        for r in range(2):
            total = sums_v[z, r, at, :].astype(f32)
            if bits:
                total = total + sums_in[count - 2, r, at, :].astype(f32)
            kv_v[r, at, :] = (inv_f[at, :1] * total).astype(bf16)
        return 0

    lax.fori_loop(0, tokens // row_tile, head_tile, 0)
    stores.append(load(kv_v.at[0], keys_out))
    stores.append(load(kv_v.at[1], values_out))
    finish(parts - 1)
    for copy in sent:
        copy.wait_send()
    for copy in stores:
        copy.wait()


def run_layer(count, sections, arr, kept, ret, gain, wk, wv, dnk, dnv, upk, upv, ck, cv):
    rows, width = kept.shape
    depth, wide = wk.shape
    tokens, heads = ck.shape
    rank = upk.shape[0]
    copies = 4 * (count - 1) + (count - 1) + halves * count + count + 1
    copies += parts * (count - 1) + 3 * (count - 1)
    hbm = pl.BlockSpec(memory_space=pl.ANY)
    landing = max(count - 1, 1)
    return pl.pallas_call(
        functools.partial(layer_kernel, count, sections),
        in_specs=[pl.BlockSpec(memory_space=pltpu.VMEM)] + [hbm] * 11,
        out_specs=[hbm] * 7,
        out_shape=[
            jax.ShapeDtypeStruct((tokens, heads), bf16),
            jax.ShapeDtypeStruct((tokens, heads), bf16),
            jax.ShapeDtypeStruct((rows, width), bf16),
            jax.ShapeDtypeStruct((rank, depth), f32),
            jax.ShapeDtypeStruct((rank, depth), f32),
            jax.ShapeDtypeStruct((rank, heads), f32),
            jax.ShapeDtypeStruct((rank, heads), f32),
        ],
        scratch_shapes=[
            pltpu.VMEM((depth, wide), bf16),
            pltpu.VMEM((depth, wide), bf16),
            pltpu.VMEM((tokens, wide), bf16),
            pltpu.VMEM((tokens, wide), bf16),
            pltpu.VMEM((rank, wide), bf16),
            pltpu.VMEM((rank, wide), bf16),
            pltpu.VMEM((count, 2 * rank, depth), bf16),
            pltpu.VMEM((rows, width), bf16),
            pltpu.VMEM((rows, width), bf16),
            pltpu.VMEM((rows, width), bf16),
            pltpu.VMEM((count, rows, depth), bf16),
            pltpu.VMEM((rows, lanes), f32),
            pltpu.VMEM((2 * count, 8, rows), f32),
            pltpu.VMEM((tokens, lanes), f32),
            pltpu.VMEM((rows, lanes), f32),
            pltpu.VMEM((tokens, 2 * rank), f32),
            pltpu.VMEM((2 * rank, tokens), f32),
            pltpu.VMEM((rows, 2 * rank), bf16),
            pltpu.VMEM((count, rows, depth), bf16),
            pltpu.VMEM((count, rows, depth), bf16),
            pltpu.VMEM((rows, depth), bf16),
            pltpu.VMEM((count, 2 * rank, depth), bf16),
            pltpu.VMEM((landing, 2 * rank, depth), bf16),
            pltpu.VMEM((count, 2 * rank, rows), f32),
            pltpu.VMEM((count, 2, tokens, heads), bf16),
            pltpu.VMEM((landing, 2, tokens, heads), bf16),
            pltpu.VMEM((2, tokens, heads), bf16),
            pltpu.VMEM((2 * rank, depth), f32),
            pltpu.VMEM((2, rank, heads), f32),
            pltpu.SemaphoreType.DMA((copies,)),
            pltpu.SemaphoreType.DMA((copies,)),
            pltpu.SemaphoreType.DMA((10 + 6 + parts,)),
        ],
        compiler_params=pltpu.CompilerParams(
            has_side_effects=True, vmem_limit_bytes=67043328
        ),
        cost_estimate=pl.CostEstimate(
            flops=8 * tokens * depth * wide, bytes_accessed=4 * depth * wide, transcendentals=0
        ),
        name="layer",
    )(gain, arr, kept, ret, wk, wv, dnk, dnv, upk, upv, ck, cv)


def on_device(
    arriving,
    kept_input,
    returning,
    norm_gain,
    key_weight,
    value_weight,
    key_down,
    value_down,
    key_up,
    value_up,
    key_cot,
    value_cot,
):
    keys, values, input_grad, dgk, dgv, ugk, ugv = run_layer(
        lax.axis_size("tensor"),
        lax.axis_size("section"),
        arriving[0],
        kept_input[0],
        returning[0],
        norm_gain,
        key_weight[0],
        value_weight[0],
        key_down[0].T,
        value_down[0].T,
        key_up[0],
        value_up[0],
        key_cot[0],
        value_cot[0],
    )
    return (
        keys[None],
        values[None],
        input_grad[None],
        dgk.T[None],
        dgv.T[None],
        ugk[None],
        ugv[None],
    )


def solution(mesh):
    return jax.shard_map(
        on_device,
        mesh=mesh,
        in_specs=(
            P("section", "tensor", None),
            P("section", "tensor", None),
            P("section", "tensor", None),
            P("section", None),
            P("section", "tensor", None),
            P("section", "tensor", None),
            P("section", "tensor", None),
            P("section", "tensor", None),
            P("section", None, "tensor"),
            P("section", None, "tensor"),
            P("section", None, "tensor"),
            P("section", None, "tensor"),
        ),
        out_specs=(
            P("section", None, "tensor"),
            P("section", None, "tensor"),
            P("section", "tensor", None),
            P("section", "tensor", None),
            P("section", "tensor", None),
            P("section", None, "tensor"),
            P("section", None, "tensor"),
        ),
        check_vma=False,
    )
```

profile of v0, /device:TPU:0, one launch (start us, length us, event | category | flops | bytes accessed | tf_op | source)
XLA Modules:
  0.0 289.8 jit_solution(9537617711483947086)
XLA Ops:
  0.6 278.5 %layer.1 = (bf16[512,256]{1,0:T(8,128)(2,1)}, bf16[512,256]{1,0:T(8,128)(2,1)}, bf16[128,16384]{1,0:T(8,128)(2,1)}, f32[16,4096]{1,0:T(8,128)}, f32[16,4096]{1,0...) custom-call(bf16[1,16384]{1,0:T(2,128)(2,1)} %gain_ref.1, bf16[128,16384]{1,0:T(8,128)(2,1)} %bitcast.35, ...), custom_call_target="tpu_custom_call" | custom-call | flops 17179869184 | bytes 16777216 | tf_op jit(solution)/shard_map/layer/pallas_call | solution.py:428
  279.2 1.7 copy.26
  280.8 1.7 copy.27
  282.5 0.0 copy-start.1
  282.5 0.0 copy-start
  282.5 0.0 copy-start.3
  282.5 0.0 copy-start.2
  282.5 4.6 %copy.28 = bf16[1,128,16384]{2,1,0:T(8,128)(2,1)} copy(bf16[1,128,16384]{2,1,0:T(8,128)(2,1)} %bitcast.26) | data formatting | bytes 8388608
  287.1 0.0 copy-done.1
  287.1 0.7 copy.29
  287.8 0.0 copy-done
  287.8 0.7 copy.30
  288.5 0.0 copy-done.3
  288.5 0.6 copy.31
  289.2 0.0 copy-done.2
  289.2 0.6 copy.32
Async XLA Ops:
  282.5 4.6 %copy-start.1 = (f32[16,4096]{1,0:T(8,128)S(1)}, f32[16,4096]{1,0:T(8,128)}, u32[]{:S(2)}) copy-start(f32[16,4096]{1,0:T(8,128)} %get-tuple-element.17) | copy-start | bytes 786436
  282.5 5.3 %copy-start = (f32[16,4096]{1,0:T(8,128)S(1)}, f32[16,4096]{1,0:T(8,128)}, u32[]{:S(2)}) copy-start(f32[16,4096]{1,0:T(8,128)} %get-tuple-element.18) | copy-start | bytes 786436
  282.5 6.0 %copy-start.3 = (f32[16,256]{1,0:T(8,128)S(1)}, f32[16,256]{1,0:T(8,128)}, u32[]{:S(2)}) copy-start(f32[16,256]{1,0:T(8,128)} %get-tuple-element.19) | copy-start | bytes 49156
  282.5 6.7 %copy-start.2 = (f32[16,256]{1,0:T(8,128)S(1)}, f32[16,256]{1,0:T(8,128)}, u32[]{:S(2)}) copy-start(f32[16,256]{1,0:T(8,128)} %get-tuple-element.20) | copy-start | bytes 49156
where the time goes:
time: 293 us; the launch traced here: 290 us
  Pallas kernels  279 us (95%)
  local copies, waits for them, and re-layouts  10.6 us (4%)
    pallas_call x1, Pallas kernels, run_layer(): pl.pallas_call(functools.partial(layer_kernel, count, sections), in_specs...  279 us
    unnamed x15, local copies, waits for them, and re-layouts  10.6 us

commit v1 on v0

--- a/solution.py
+++ b/solution.py
@@ -117,10 +117,8 @@
 
     sent = []
 
-    def send(src, dst, section, tensor):
-        k = used[0]
-        used[0] += 1
-        copy = pltpu.make_async_remote_copy(
+    def remote(src, dst, k, section, tensor):
+        return pltpu.make_async_remote_copy(
             src_ref=src,
             dst_ref=dst,
             send_sem=send_sem.at[k],
@@ -128,6 +126,10 @@
             device_id=(section, tensor),
             device_id_type=MESH,
         )
+
+    def send(src, dst, section, tensor):
+        copy = remote(src, dst, used[0], section, tensor)
+        used[0] += 1
         copy.start()
         sent.append(copy)
         return copy
@@ -139,7 +141,6 @@
         return pl.ds(pl.multiple_of(q * depth, depth), depth)
 
     bits = bits_up(count)
-    down_bits = list(reversed(bits))
     own = [
         load(ck, cotk.at[:, head_cols(z)]),
         load(cv, cotv.at[:, head_cols(z)]),
@@ -151,39 +152,70 @@
     kept_load = load(kept, kept_v)
     weights = [load(wk, wk_v), load(wv, wv_v)]
 
-    def gather_stage(held, bit, kinds):
-        to = flip(z, bit)
-        copies = []
-        for h in held:
-            q = flip(z, h)
-            if "c" in kinds:
-                for src, dst in ((ck, cotk), (cv, cotv), (upk, upk_v), (upv, upv_v)):
-                    block = dst.at[:, head_cols(q)]
-                    copies.append(send(block if h else src, block, s, to))
-            if "d" in kinds:
-                copies.append(send(dn_v.at[q], dn_v.at[q], s, to))
-        return copies
+    def inside(q):
+        return (q >= 0) & (q < count)
+
+    head_kinds = ((ck, cotk), (cv, cotv), (upk, upk_v), (upv, upv_v))
+    guarded = []
+
+    def relay(step, kinds):
+        landing = []
+        for way in (1, -1):
+            q, to, come = z - way * (step - 1), z + way, z - way * step
+            going = inside(q) & inside(to)
+            for kind in kinds:
+                if kind == 4:
+                    src, dst, got = dn_v.at[q], dn_v.at[q], dn_v.at[come]
+                else:
+                    first, buf = head_kinds[kind]
+                    dst, got = buf.at[:, head_cols(q)], buf.at[:, head_cols(come)]
+                    src = first if step == 1 else dst
+                k = used[0]
+                used[0] += 1
+                out = remote(src, dst, k, s, to)
+                pl.when(going)(out.start)
+                guarded.append((going, out))
+                landing.append((kind, inside(come), remote(got, got, k, s, z)))
+        return landing
+
+    def landed(landing, kinds):
+        for kind, coming, copy in landing:
+            if kind in kinds:
+                pl.when(coming)(copy.wait_recv)
 
     half = rows // halves
-
-    def send_arriving(j, i):
+    ends = (z == 0) | (z == count - 1)
+
+    def arriving(j, i):
         q = flip(z, j)
         at = pl.ds(i * half, half)
-        return send(arr.at[at, depth_cols(q)], x_v.at[z, at], ahead, q)
-
-    far = [j for j in range(count) if j >= max(bits[-1], 1)] if bits else []
+        copy = remote(arr.at[at, depth_cols(q)], x_v.at[z, at], used[0], ahead, q)
+        used[0] += 1
+        sent.append(copy)
+        return copy
+
+    far = list(range(max(bits[-1], 1), count)) if bits else []
     near = [j for j in range(1, count) if j not in far]
-    arrivals = {}
-    held = [0]
-    stage = gather_stage(held, down_bits[0], "c") if bits else []
+    arrivals = {(j, i): arriving(j, i) for j in range(count) for i in range(halves)}
+
+    def start_near():
+        for i in range(halves):
+            for j in near:
+                arrivals[j, i].start()
+
+    def start_far(i):
+        for j in far:
+            arrivals[j, i].start()
+
+    heads_only, down_only = (0, 1, 2, 3), (4,)
+    landing = relay(1, heads_only) if bits else []
     for i in range(halves):
-        arrivals[0, i] = send_arriving(0, i)
-    for j in far:
-        arrivals[j, 0] = send_arriving(j, 0)
+        arrivals[0, i].start()
     returned = send(ret, back_v, behind, z)
     for copy in own_down:
         copy.wait()
-    down_stage = gather_stage(held, down_bits[0], "d") if bits else []
+    landing += relay(1, down_only) if bits else []
+    pl.when(ends)(start_near)
 
     arr_load.wait()
 
@@ -206,29 +238,22 @@
         inv_b[at, :] = jnp.broadcast_to(inverse, (row_tile, lanes))
         return 0
 
-    lax.fori_loop(0, rows // row_tile, kept_stats, 0)
-
-    for bit in down_bits[:1]:
-        for copy in stage:
-            copy.wait_recv()
-        held = held + [h ^ bit for h in held]
-    waiting = list(down_stage)
-    for bit in down_bits[1:]:
-        stage = gather_stage(held, bit, "c")
-        if bit == down_bits[1]:
-            for i in range(1, halves):
-                for j in far:
-                    arrivals[j, i] = send_arriving(j, i)
-        for copy in waiting:
-            copy.wait_recv()
-        waiting = gather_stage(held, bit, "d")
-        for copy in stage:
-            copy.wait_recv()
-        held = held + [h ^ bit for h in held]
-    for i in range(halves):
-        for j in near + far:
-            if (j, i) not in arrivals:
-                arrivals[j, i] = send_arriving(j, i)
+    for step in range(1, count):
+        landed(landing, heads_only)
+        ahead_of = relay(step + 1, heads_only) if step + 1 < count else []
+        landed(landing, down_only)
+        ahead_of += relay(step + 1, down_only) if step + 1 < count else []
+        landing = ahead_of
+        if step <= halves:
+            start_far(step - 1)
+        if step == 1:
+            lax.fori_loop(0, rows // row_tile, kept_stats, 0)
+        if step == max(count - 2, 1):
+            pl.when(jnp.logical_not(ends))(start_near)
+    for i in range(max(count - 1, 0), halves):
+        start_far(i)
+    if count == 1:
+        lax.fori_loop(0, rows // row_tile, kept_stats, 0)
     for copy in own + weights:
         copy.wait()
 
@@ -257,8 +282,7 @@
             q = flip(z, j)
             branches[j, i] = send(bo_v.at[q, at], bi_v.at[z, at], s, q)
 
-    for i in range(parts // 2):
-        send_branch(i)
+    send_branch(0)
 
     def own_branch(i, _):
         at = pl.ds(pl.multiple_of(i * row_tile, row_tile), row_tile)
@@ -267,8 +291,6 @@
 
     lax.fori_loop(0, rows // row_tile, own_branch, 0)
 
-    for copy in waiting:
-        copy.wait_recv()
     mine = adt_v[:, pl.ds(pl.multiple_of(z * rows, rows), rows)].astype(bf16)
 
     km_v[z] = jnp.zeros((2 * rank, rows), f32)
@@ -339,14 +361,13 @@
     for k, bit in enumerate(bits):
         stage = scatter_stage(sums_v, sums_in, bit)
         if k == 0:
-            send_branch(parts // 2)
+            for i in range(1, parts):
+                send_branch(i)
         scatter_add(dp_v, dp_in, bit, down_stage)
         if k + 1 < len(bits):
             down_stage = scatter_stage(dp_v, dp_in, bits[k + 1])
         if k + 1 < len(bits):
             scatter_add(sums_v, sums_in, bit, stage)
-    for i in range(parts // 2 + 1, parts):
-        send_branch(i)
 
     dg_v[...] = dp_v[z].astype(f32)
     stores.append(load(dg_v.at[:rank], dgk_out))
@@ -391,7 +412,7 @@
         at = pl.ds(i * part, part)
         stores.append(load(arr_v.at[at], grad_out.at[at]))
 
-    for i in range(parts - 1):
+    for i in range(parts):
         finish(i)
 
     if bits:
@@ -409,9 +430,10 @@
     lax.fori_loop(0, tokens // row_tile, head_tile, 0)
     stores.append(load(kv_v.at[0], keys_out))
     stores.append(load(kv_v.at[1], values_out))
-    finish(parts - 1)
     for copy in sent:
         copy.wait_send()
+    for going, copy in guarded:
+        pl.when(going)(copy.wait_send)
     for copy in stores:
         copy.wait()
 
@@ -421,7 +443,7 @@
     depth, wide = wk.shape
     tokens, heads = ck.shape
     rank = upk.shape[0]
-    copies = 4 * (count - 1) + (count - 1) + halves * count + count + 1
+    copies = 10 * (count - 1) + halves * count + count + 1
     copies += parts * (count - 1) + 3 * (count - 1)
     hbm = pl.BlockSpec(memory_space=pl.ANY)
     landing = max(count - 1, 1)

time: 293 us -> 278 us (0.949); the launches traced: 290 us -> 278 us
  Pallas kernels: 279 us -> 267 us
    pallas_call x1, Pallas kernels: 279 us -> 267 us  [run_layer(): pl.pallas_call(functools.partial(layer_kernel, count, sections), in_specs...]
where the time goes in v1:
time: 278 us
  Pallas kernels  267 us (96%)
  local copies, waits for them, and re-layouts  10.6 us (4%)
    pallas_call x1, Pallas kernels, run_layer(): pl.pallas_call(functools.partial(layer_kernel, count, sections), in_specs...  267 us
    unnamed x15, local copies, waits for them, and re-layouts  10.6 us

profile of v1, /device:TPU:0, one launch (start us, length us, event | category | flops | bytes accessed | tf_op | source)
XLA Modules:
  0.0 277.9 jit_solution(9664639151746590506)
XLA Ops:
  0.6 266.6 %layer.1 = (bf16[512,256]{1,0:T(8,128)(2,1)}, bf16[512,256]{1,0:T(8,128)(2,1)}, bf16[128,16384]{1,0:T(8,128)(2,1)}, f32[16,4096]{1,0:T(8,128)}, f32[16,4096]{1,0...) custom-call(bf16[1,16384]{1,0:T(2,128)(2,1)} %gain_ref.1, bf16[128,16384]{1,0:T(8,128)(2,1)} %bitcast.35, ...), custom_call_target="tpu_custom_call" | custom-call | flops 17179869184 | bytes 16777216 | tf_op jit(solution)/shard_map/layer/pallas_call | solution.py:450
  267.3 1.7 copy.26
  268.9 1.7 copy.27
  270.6 0.0 copy-start.1
  270.6 0.0 copy-start
  270.6 0.0 copy-start.3
  270.6 0.0 copy-start.2
  270.6 4.6 %copy.28 = bf16[1,128,16384]{2,1,0:T(8,128)(2,1)} copy(bf16[1,128,16384]{2,1,0:T(8,128)(2,1)} %bitcast.26) | data formatting | bytes 8388608
  275.3 0.0 copy-done.1
  275.3 0.7 copy.29
  276.0 0.0 copy-done
  276.0 0.7 copy.30
  276.7 0.0 copy-done.3
  276.7 0.6 copy.31
  277.3 0.0 copy-done.2
  277.3 0.6 copy.32
Async XLA Ops:
  270.6 4.6 %copy-start.1 = (f32[16,4096]{1,0:T(8,128)S(1)}, f32[16,4096]{1,0:T(8,128)}, u32[]{:S(2)}) copy-start(f32[16,4096]{1,0:T(8,128)} %get-tuple-element.17) | copy-start | bytes 786436
  270.6 5.3 %copy-start = (f32[16,4096]{1,0:T(8,128)S(1)}, f32[16,4096]{1,0:T(8,128)}, u32[]{:S(2)}) copy-start(f32[16,4096]{1,0:T(8,128)} %get-tuple-element.18) | copy-start | bytes 786436
  270.6 6.0 %copy-start.3 = (f32[16,256]{1,0:T(8,128)S(1)}, f32[16,256]{1,0:T(8,128)}, u32[]{:S(2)}) copy-start(f32[16,256]{1,0:T(8,128)} %get-tuple-element.19) | copy-start | bytes 49156
  270.6 6.7 %copy-start.2 = (f32[16,256]{1,0:T(8,128)S(1)}, f32[16,256]{1,0:T(8,128)}, u32[]{:S(2)}) copy-start(f32[16,256]{1,0:T(8,128)} %get-tuple-element.20) | copy-start | bytes 49156

commit v2 on v1

--- a/solution.py
+++ b/solution.py
@@ -16,6 +16,9 @@
 parts = 4
 halves = 2
 row_tile = 16
+kernel_mib = 55
+store_mib = 16
+store_tile = 128
 
 
 def flip(z, mask):
@@ -47,7 +50,7 @@
 def layer_kernel(
     count,
     sections,
-    gain_ref,
+    gain,
     arr,
     kept,
     ret,
@@ -59,13 +62,15 @@
     upv,
     ck,
     cv,
-    keys_out,
-    values_out,
+    own_out,
+    sum_out,
+    inv_f,
     grad_out,
     dgk_out,
     dgv_out,
     ugk_out,
     ugv_out,
+    gain_ref,
     wk_v,
     wv_v,
     cotk,
@@ -79,7 +84,6 @@
     x_v,
     inv_t,
     inv_in,
-    inv_f,
     inv_b,
     ad_v,
     adt_v,
@@ -89,12 +93,10 @@
     nb_v,
     dp_v,
     dp_in,
+    km_sum,
     km_v,
     sums_v,
     sums_in,
-    kv_v,
-    dg_v,
-    ug_v,
     send_sem,
     recv_sem,
     local_sem,
@@ -140,6 +142,13 @@
     def depth_cols(q):
         return pl.ds(pl.multiple_of(q * depth, depth), depth)
 
+    greet = [(s, flip(z, j)) for j in range(1, count)]
+    greet += [(behind, flip(z, j)) for j in range(count)] + [(ahead, z)]
+    entry = pltpu.get_barrier_semaphore()
+    for peer in greet:
+        pl.semaphore_signal(entry, inc=1, device_id=peer, device_id_type=MESH)
+    pl.semaphore_wait(entry, len(greet))
+
     bits = bits_up(count)
     own = [
         load(ck, cotk.at[:, head_cols(z)]),
@@ -150,7 +159,7 @@
     own_down = [load(dnk, dn_v.at[z, :rank]), load(dnv, dn_v.at[z, rank:])]
     arr_load = load(arr, arr_v)
     kept_load = load(kept, kept_v)
-    weights = [load(wk, wk_v), load(wv, wv_v)]
+    weights = [load(gain, gain_ref), load(wk, wk_v), load(wv, wv_v)]
 
     def inside(q):
         return (q >= 0) & (q < count)
@@ -293,7 +302,7 @@
 
     mine = adt_v[:, pl.ds(pl.multiple_of(z * rows, rows), rows)].astype(bf16)
 
-    km_v[z] = jnp.zeros((2 * rank, rows), f32)
+    km_sum[...] = jnp.zeros((2 * rank, rows), f32)
 
     def kept_block(j, _):
         inverse = inv_b[:, :1]
@@ -306,18 +315,25 @@
             return 0
 
         lax.fori_loop(0, depth // tile, normalize, 0)
-        km_v[z] += dot_nt(dn_v[j], nb_v[...])
+        km_sum[...] += dot_nt(dn_v[j], nb_v[...])
         dp_v[j] = dot_nn(mine, nb_v[...]).astype(bf16)
         return 0
 
     lax.fori_loop(0, count, kept_block, 0)
+    km_v[z] = (adapter_scale * km_sum[...]).astype(bf16)
     mids = [send(km_v.at[z], km_v.at[z], s, flip(z, j)) for j in range(1, count)]
+
+    def down_slot(k):
+        return dp_in.at[k]
+
+    def sum_slot(k):
+        return sum_out if k == count - 2 else sums_in.at[k]
 
     def scatter_stage(buf, landing, bit):
         to = flip(z, bit)
         offset = sum(count // (2 * b) for b in bits if b < bit)
         return [
-            send(buf.at[flip(z, bit ^ m)], landing.at[offset + k], s, to)
+            send(buf.at[flip(z, bit ^ m)], landing(offset + k), s, to)
             for k, m in enumerate(range(0, count, 2 * bit))
         ]
 
@@ -326,10 +342,9 @@
         for k, m in enumerate(range(0, count, 2 * bit)):
             copies[k].wait_recv()
             q = flip(z, m)
-            buf[q] = (buf[q].astype(f32) + landing[offset + k].astype(f32)).astype(bf16)
-
-    stores = []
-    down_stage = scatter_stage(dp_v, dp_in, bits[0]) if bits else []
+            buf[q] = (buf[q].astype(f32) + landing(offset + k)[...].astype(f32)).astype(bf16)
+
+    down_stage = scatter_stage(dp_v, down_slot, bits[0]) if bits else []
 
     def head_block(q):
         gain_cols = depth_cols(z)
@@ -359,34 +374,32 @@
             arrivals[j, i].wait_recv()
         head_block(flip(z, j))
     for k, bit in enumerate(bits):
-        stage = scatter_stage(sums_v, sums_in, bit)
+        stage = scatter_stage(sums_v, sum_slot, bit)
         if k == 0:
             for i in range(1, parts):
                 send_branch(i)
-        scatter_add(dp_v, dp_in, bit, down_stage)
+        scatter_add(dp_v, down_slot, bit, down_stage)
         if k + 1 < len(bits):
-            down_stage = scatter_stage(dp_v, dp_in, bits[k + 1])
+            down_stage = scatter_stage(dp_v, down_slot, bits[k + 1])
         if k + 1 < len(bits):
-            scatter_add(sums_v, sums_in, bit, stage)
-
-    dg_v[...] = dp_v[z].astype(f32)
-    stores.append(load(dg_v.at[:rank], dgk_out))
-    stores.append(load(dg_v.at[rank:], dgv_out))
+            scatter_add(sums_v, sum_slot, bit, stage)
+
+    dgk_out[...] = dp_v[z, :rank].astype(f32)
+    dgv_out[...] = dp_v[z, rank:].astype(f32)
     for copy in mids:
         copy.wait_recv()
     for r, cot in enumerate((cotk, cotv)):
         total = jnp.zeros((rank, heads), f32)
         for q in range(count):
-            mid = (adapter_scale * km_v[q, r * rank : (r + 1) * rank, :]).astype(bf16)
+            mid = km_v[q, r * rank : (r + 1) * rank, :]
             total = total + dot_nn(mid, cot[q * rows : (q + 1) * rows, head_cols(z)])
-        ug_v[r] = total
-    stores.append(load(ug_v.at[0], ugk_out))
-    stores.append(load(ug_v.at[1], ugv_out))
+        (ugk_out, ugv_out)[r][...] = total
     for copy in inverses:
         copy.wait_recv()
     for q in range(count):
         spread = jnp.broadcast_to(inv_in[count + q, :1, :], (lanes, rows)).T
         inv_f[q * rows : (q + 1) * rows, :] = spread
+    own_out[...] = sums_v[z]
     returned.wait_recv()
 
     def grad_tile(i, _):
@@ -402,40 +415,25 @@
             cols = slice(j * depth, (j + 1) * depth)
             scaled = gain_ref[:, cols].astype(f32) * bi_v[j, at, :].astype(f32)
             value = back_v[at, cols].astype(f32) + inverse * scaled - kept_v[at, cols].astype(f32) * pull
-            arr_v[at, cols] = value.astype(bf16)
+            grad_out[at, cols] = value.astype(bf16)
         return 0
 
     def finish(i):
         for j in others:
             branches[j, i].wait_recv()
         lax.fori_loop(i * part // row_tile, (i + 1) * part // row_tile, grad_tile, 0)
-        at = pl.ds(i * part, part)
-        stores.append(load(arr_v.at[at], grad_out.at[at]))
 
     for i in range(parts):
         finish(i)
 
     if bits:
         stage[0].wait_recv()
-
-    def head_tile(i, _):
-        at = pl.ds(pl.multiple_of(i * row_tile, row_tile), row_tile)
-        for r in range(2):
-            total = sums_v[z, r, at, :].astype(f32)
-            if bits:
-                total = total + sums_in[count - 2, r, at, :].astype(f32)
-            kv_v[r, at, :] = (inv_f[at, :1] * total).astype(bf16)
-        return 0
-
-    lax.fori_loop(0, tokens // row_tile, head_tile, 0)
-    stores.append(load(kv_v.at[0], keys_out))
-    stores.append(load(kv_v.at[1], values_out))
+    else:
+        sum_out[...] = jnp.zeros(sum_out.shape, bf16)
     for copy in sent:
         copy.wait_send()
     for going, copy in guarded:
         pl.when(going)(copy.wait_send)
-    for copy in stores:
-        copy.wait()
 
 
 def run_layer(count, sections, arr, kept, ret, gain, wk, wv, dnk, dnv, upk, upv, ck, cv):
@@ -449,18 +447,20 @@
     landing = max(count - 1, 1)
     return pl.pallas_call(
         functools.partial(layer_kernel, count, sections),
-        in_specs=[pl.BlockSpec(memory_space=pltpu.VMEM)] + [hbm] * 11,
-        out_specs=[hbm] * 7,
+        in_specs=[hbm] * 12,
+        out_specs=[pl.BlockSpec(memory_space=pltpu.VMEM)] * 8,
         out_shape=[
-            jax.ShapeDtypeStruct((tokens, heads), bf16),
-            jax.ShapeDtypeStruct((tokens, heads), bf16),
-            jax.ShapeDtypeStruct((rows, width), bf16),
-            jax.ShapeDtypeStruct((rank, depth), f32),
-            jax.ShapeDtypeStruct((rank, depth), f32),
-            jax.ShapeDtypeStruct((rank, heads), f32),
-            jax.ShapeDtypeStruct((rank, heads), f32),
+            pltpu.VMEM((2, tokens, heads), bf16),
+            pltpu.VMEM((2, tokens, heads), bf16),
+            pltpu.VMEM((tokens, lanes), f32),
+            pltpu.VMEM((rows, width), bf16),
+            pltpu.VMEM((rank, depth), f32),
+            pltpu.VMEM((rank, depth), f32),
+            pltpu.VMEM((rank, heads), f32),
+            pltpu.VMEM((rank, heads), f32),
         ],
         scratch_shapes=[
+            pltpu.VMEM((1, width), bf16),
             pltpu.VMEM((depth, wide), bf16),
             pltpu.VMEM((depth, wide), bf16),
             pltpu.VMEM((tokens, wide), bf16),
@@ -474,7 +474,6 @@
             pltpu.VMEM((count, rows, depth), bf16),
             pltpu.VMEM((rows, lanes), f32),
             pltpu.VMEM((2 * count, 8, rows), f32),
-            pltpu.VMEM((tokens, lanes), f32),
             pltpu.VMEM((rows, lanes), f32),
             pltpu.VMEM((tokens, 2 * rank), f32),
             pltpu.VMEM((2 * rank, tokens), f32),
@@ -484,24 +483,64 @@
             pltpu.VMEM((rows, depth), bf16),
             pltpu.VMEM((count, 2 * rank, depth), bf16),
             pltpu.VMEM((landing, 2 * rank, depth), bf16),
-            pltpu.VMEM((count, 2 * rank, rows), f32),
+            pltpu.VMEM((2 * rank, rows), f32),
+            pltpu.VMEM((count, 2 * rank, rows), bf16),
             pltpu.VMEM((count, 2, tokens, heads), bf16),
-            pltpu.VMEM((landing, 2, tokens, heads), bf16),
-            pltpu.VMEM((2, tokens, heads), bf16),
-            pltpu.VMEM((2 * rank, depth), f32),
-            pltpu.VMEM((2, rank, heads), f32),
+            pltpu.VMEM((max(count - 2, 1), 2, tokens, heads), bf16),
             pltpu.SemaphoreType.DMA((copies,)),
             pltpu.SemaphoreType.DMA((copies,)),
-            pltpu.SemaphoreType.DMA((10 + 6 + parts,)),
+            pltpu.SemaphoreType.DMA((11,)),
         ],
         compiler_params=pltpu.CompilerParams(
-            has_side_effects=True, vmem_limit_bytes=67043328
+            has_side_effects=True, collective_id=0, vmem_limit_bytes=kernel_mib * 2**20
         ),
         cost_estimate=pl.CostEstimate(
             flops=8 * tokens * depth * wide, bytes_accessed=4 * depth * wide, transcendentals=0
         ),
         name="layer",
     )(gain, arr, kept, ret, wk, wv, dnk, dnv, upk, upv, ck, cv)
+
+
+def store_kernel(cuts, own, got, inv, grad, dgk, dgv, ugk, ugv, *refs):
+    outs, (keys_v, values_v, sem) = refs[:7], refs[7:]
+    copies = []
+
+    def store(src, dst):
+        copies.append(pltpu.make_async_copy(src, dst, sem.at[len(copies)]))
+        copies[-1].start()
+
+    step = grad.shape[0] // cuts
+    for i in range(cuts):
+        at = pl.ds(i * step, step)
+        store(grad.at[at], outs[2].at[at])
+    for src, dst in zip((dgk, dgv, ugk, ugv), outs[3:]):
+        store(src, dst)
+    for r, head in enumerate((keys_v, values_v)):
+
+        cut = min(store_tile, head.shape[0])
+        for i in range(0, head.shape[0], cut):
+            at = slice(i, i + cut)
+            total = own[r, at, :].astype(f32) + got[r, at, :].astype(f32)
+            head[at, :] = (inv[at, :1] * total).astype(bf16)
+        store(head, outs[r])
+    for copy in copies:
+        copy.wait()
+
+
+def store(results):
+    own, _, _, *rest = results
+    head = jax.ShapeDtypeStruct(own.shape[1:], bf16)
+    cuts = 4
+    return pl.pallas_call(
+        functools.partial(store_kernel, cuts),
+        in_specs=[pl.BlockSpec(memory_space=pltpu.VMEM)] * len(results),
+        out_specs=[pl.BlockSpec(memory_space=pl.ANY)] * 7,
+        out_shape=[head, head] + [jax.ShapeDtypeStruct(x.shape, x.dtype) for x in rest],
+        scratch_shapes=[pltpu.VMEM(head.shape, bf16)] * 2
+        + [pltpu.SemaphoreType.DMA((cuts + 6,))],
+        compiler_params=pltpu.CompilerParams(vmem_limit_bytes=store_mib * 2**20),
+        name="store",
+    )(*results)
 
 
 def on_device(
@@ -518,7 +557,7 @@
     key_cot,
     value_cot,
 ):
-    keys, values, input_grad, dgk, dgv, ugk, ugv = run_layer(
+    keys, values, input_grad, dgk, dgv, ugk, ugv = store(run_layer(
         lax.axis_size("tensor"),
         lax.axis_size("section"),
         arriving[0],
@@ -533,7 +572,7 @@
         value_up[0],
         key_cot[0],
         value_cot[0],
-    )
+    ))
     return (
         keys[None],
         values[None],

time: 278 us -> 262 us (0.942)
  local copies, waits for them, and re-layouts: 10.6 us -> 0 us
  Pallas kernels: 267 us -> 261 us
    unnamed x15 -> x0, local copies, waits for them, and re-layouts: 10.6 us -> none
    pallas_call x1, Pallas kernels: 267 us -> 259 us  [run_layer(): pl.pallas_call(functools.partial(layer_kernel, count, sections), in_specs...]
where the time goes in v2:
time: 262 us
  Pallas kernels  261 us (100%)
    pallas_call x1, Pallas kernels, run_layer(): pl.pallas_call(functools.partial(layer_kernel, count, sections), in_specs...  259 us

profile of v2, /device:TPU:0, one launch (start us, length us, event | category | flops | bytes accessed | tf_op | source)
XLA Modules:
  0.0 261.7 jit_solution(12688774320961331220)
XLA Ops:
  0.6 258.6 %layer.1 = (bf16[2,512,256]{2,1,0:T(8,128)(2,1)S(1)}, bf16[2,512,256]{2,1,0:T(8,128)(2,1)S(1)}, f32[512,128]{1,0:T(8,128)S(1)}, bf16[128,16384]{1,0:T(8,128)(2,1...) custom-call(bf16[1,16384]{1,0:T(2,128)(2,1)} %gain.1, ...), custom_call_target="tpu_custom_call" | custom-call | flops 17179869184 | bytes 16777216 | tf_op jit(solution)/shard_map/layer/pallas_call | solution.py:448
  259.2 2.4 store.1

commit v3 on v2

--- a/solution.py
+++ b/solution.py
@@ -13,7 +13,8 @@
 f32 = jnp.float32
 MESH = pl.DeviceIdType.MESH
 lanes = 128
-parts = 4
+cuts_of_16 = (0, 4, 8, 12, 14, 16)
+parts = len(cuts_of_16) - 1
 halves = 2
 row_tile = 16
 kernel_mib = 55
@@ -129,11 +130,15 @@
             device_id_type=MESH,
         )
 
-    def send(src, dst, section, tensor):
+    def later(src, dst, section, tensor):
         copy = remote(src, dst, used[0], section, tensor)
         used[0] += 1
+        sent.append(copy)
+        return copy
+
+    def send(src, dst, section, tensor):
+        copy = later(src, dst, section, tensor)
         copy.start()
-        sent.append(copy)
         return copy
 
     def head_cols(q):
@@ -147,7 +152,6 @@
     entry = pltpu.get_barrier_semaphore()
     for peer in greet:
         pl.semaphore_signal(entry, inc=1, device_id=peer, device_id_type=MESH)
-    pl.semaphore_wait(entry, len(greet))
 
     bits = bits_up(count)
     own = [
@@ -160,11 +164,14 @@
     arr_load = load(arr, arr_v)
     kept_load = load(kept, kept_v)
     weights = [load(gain, gain_ref), load(wk, wk_v), load(wv, wv_v)]
+    for copy in own + own_down:
+        copy.wait()
+    pl.semaphore_wait(entry, len(greet))
 
     def inside(q):
         return (q >= 0) & (q < count)
 
-    head_kinds = ((ck, cotk), (cv, cotv), (upk, upk_v), (upv, upv_v))
+    head_kinds = (cotk, cotv, upk_v, upv_v)
     guarded = []
 
     def relay(step, kinds):
@@ -174,14 +181,13 @@
             going = inside(q) & inside(to)
             for kind in kinds:
                 if kind == 4:
-                    src, dst, got = dn_v.at[q], dn_v.at[q], dn_v.at[come]
+                    block, got = dn_v.at[q], dn_v.at[come]
                 else:
-                    first, buf = head_kinds[kind]
-                    dst, got = buf.at[:, head_cols(q)], buf.at[:, head_cols(come)]
-                    src = first if step == 1 else dst
+                    buf = head_kinds[kind]
+                    block, got = buf.at[:, head_cols(q)], buf.at[:, head_cols(come)]
                 k = used[0]
                 used[0] += 1
-                out = remote(src, dst, k, s, to)
+                out = remote(block, block, k, s, to)
                 pl.when(going)(out.start)
                 guarded.append((going, out))
                 landing.append((kind, inside(come), remote(got, got, k, s, z)))
@@ -198,10 +204,7 @@
     def arriving(j, i):
         q = flip(z, j)
         at = pl.ds(i * half, half)
-        copy = remote(arr.at[at, depth_cols(q)], x_v.at[z, at], used[0], ahead, q)
-        used[0] += 1
-        sent.append(copy)
-        return copy
+        return later(arr.at[at, depth_cols(q)], x_v.at[z, at], ahead, q)
 
     far = list(range(max(bits[-1], 1), count)) if bits else []
     near = [j for j in range(1, count) if j not in far]
@@ -221,8 +224,6 @@
     for i in range(halves):
         arrivals[0, i].start()
     returned = send(ret, back_v, behind, z)
-    for copy in own_down:
-        copy.wait()
     landing += relay(1, down_only) if bits else []
     pl.when(ends)(start_near)
 
@@ -263,7 +264,7 @@
         start_far(i)
     if count == 1:
         lax.fori_loop(0, rows // row_tile, kept_stats, 0)
-    for copy in own + weights:
+    for copy in weights:
         copy.wait()
 
     for r, (cot, up) in enumerate(((cotk, upk_v), (cotv, upv_v))):
@@ -281,17 +282,27 @@
         return 0
 
     lax.fori_loop(0, depth // tile, branch_tile, 0)
-    part = rows // parts
+    cuts = [rows * cut // 16 for cut in cuts_of_16]
     others = far + near
-    branches = {}
-
-    def send_branch(i):
-        at = pl.ds(i * part, part)
-        for j in others:
-            q = flip(z, j)
-            branches[j, i] = send(bo_v.at[q, at], bi_v.at[z, at], s, q)
-
-    send_branch(0)
+
+    def branch(j, i):
+        at = pl.ds(cuts[i], cuts[i + 1] - cuts[i])
+        q = flip(z, j)
+        return later(bo_v.at[q, at], bi_v.at[z, at], s, q)
+
+    branches = {(j, i): branch(j, i) for j in others for i in range(parts)}
+
+    held_back = (count - 1, parts - 1)
+
+    def send_branches(group):
+        for i in range(1, parts):
+            for j in group:
+                if group is others or (j, i) != held_back:
+                    branches[j, i].start()
+
+    for j in others:
+        branches[j, 0].start()
+    pl.when(jnp.logical_not(ends))(functools.partial(send_branches, far))
 
     def own_branch(i, _):
         at = pl.ds(pl.multiple_of(i * row_tile, row_tile), row_tile)
@@ -376,16 +387,15 @@
     for k, bit in enumerate(bits):
         stage = scatter_stage(sums_v, sum_slot, bit)
         if k == 0:
-            for i in range(1, parts):
-                send_branch(i)
-        scatter_add(dp_v, down_slot, bit, down_stage)
+            pl.when(ends)(functools.partial(send_branches, others))
+            pl.when(jnp.logical_not(ends))(functools.partial(send_branches, near))
         if k + 1 < len(bits):
+            scatter_add(dp_v, down_slot, bit, down_stage)
             down_stage = scatter_stage(dp_v, down_slot, bits[k + 1])
-        if k + 1 < len(bits):
             scatter_add(sums_v, sum_slot, bit, stage)
 
-    dgk_out[...] = dp_v[z, :rank].astype(f32)
-    dgv_out[...] = dp_v[z, rank:].astype(f32)
+    if others:
+        pl.when(jnp.logical_not(ends))(branches[held_back].start)
     for copy in mids:
         copy.wait_recv()
     for r, cot in enumerate((cotk, cotv)):
@@ -421,11 +431,15 @@
     def finish(i):
         for j in others:
             branches[j, i].wait_recv()
-        lax.fori_loop(i * part // row_tile, (i + 1) * part // row_tile, grad_tile, 0)
-
-    for i in range(parts):
+        lax.fori_loop(cuts[i] // row_tile, cuts[i + 1] // row_tile, grad_tile, 0)
+
+    for i in range(parts - 1):
         finish(i)
-
+    if bits:
+        scatter_add(dp_v, down_slot, bits[-1], down_stage)
+    dgk_out[...] = dp_v[z, :rank].astype(f32)
+    dgv_out[...] = dp_v[z, rank:].astype(f32)
+    finish(parts - 1)
     if bits:
         stage[0].wait_recv()
     else:

time: 262 us -> 260 us (level)
  Pallas kernels: 261 us -> 258 us
    pallas_call x1, Pallas kernels: 259 us -> 255 us  [run_layer(): pl.pallas_call(functools.partial(layer_kernel, count, sections), in_specs...]
where the time goes in v3:
time: 260 us; the launch traced here: 259 us
  Pallas kernels  258 us (99%)
    pallas_call x1, Pallas kernels, run_layer(): pl.pallas_call(functools.partial(layer_kernel, count, sections), in_specs...  255 us

profile of v3, /device:TPU:0, one launch (start us, length us, event | category | flops | bytes accessed | tf_op | source)
XLA Modules:
  0.0 258.7 jit_solution(10275278972425873825)
XLA Ops:
  0.6 255.5 %layer.1 = (bf16[2,512,256]{2,1,0:T(8,128)(2,1)S(1)}, bf16[2,512,256]{2,1,0:T(8,128)(2,1)S(1)}, f32[512,128]{1,0:T(8,128)S(1)}, bf16[128,16384]{1,0:T(8,128)(2,1...) custom-call(bf16[1,16384]{1,0:T(2,128)(2,1)} %gain.1, ...), custom_call_target="tpu_custom_call" | custom-call | flops 17179869184 | bytes 16777216 | tf_op jit(solution)/shard_map/layer/pallas_call | solution.py:462
  256.1 2.4 store.1

commit v4 on v3

--- a/solution.py
+++ b/solution.py
@@ -147,8 +147,8 @@
     def depth_cols(q):
         return pl.ds(pl.multiple_of(q * depth, depth), depth)
 
-    greet = [(s, flip(z, j)) for j in range(1, count)]
-    greet += [(behind, flip(z, j)) for j in range(count)] + [(ahead, z)]
+    greet = [(behind, flip(z, j)) for j in reversed(range(count))]
+    greet += [(s, flip(z, j)) for j in reversed(range(1, count))] + [(ahead, z)]
     entry = pltpu.get_barrier_semaphore()
     for peer in greet:
         pl.semaphore_signal(entry, inc=1, device_id=peer, device_id_type=MESH)
@@ -238,7 +238,9 @@
 
     lax.fori_loop(0, rows // row_tile, arr_stats, 0)
     inv_in[z] = inv_t[...].T[:8]
-    inverses = [send(inv_in.at[z], inv_in.at[z + count], ahead, flip(z, j)) for j in range(count)]
+    inverses = [
+        send(inv_in.at[z, :1], inv_in.at[z + count, :1], ahead, flip(z, j)) for j in range(count)
+    ]
     kept_load.wait()
 
     def kept_stats(i, _):

time: 260 us -> 260 us (level)
  no operation moved by 1% of the time
where the time goes in v4:
time: 260 us; the launch traced here: 258 us
  Pallas kernels  258 us (99%)
    pallas_call x1, Pallas kernels, run_layer(): pl.pallas_call(functools.partial(layer_kernel, count, sections), in_specs...  255 us

profile of v4, /device:TPU:0, one launch (start us, length us, event | category | flops | bytes accessed | tf_op | source)
XLA Modules:
  0.0 258.5 jit_solution(6964897068414438315)
XLA Ops:
  0.6 255.2 %layer.1 = (bf16[2,512,256]{2,1,0:T(8,128)(2,1)S(1)}, bf16[2,512,256]{2,1,0:T(8,128)(2,1)S(1)}, f32[512,128]{1,0:T(8,128)S(1)}, bf16[128,16384]{1,0:T(8,128)(2,1...) custom-call(bf16[1,16384]{1,0:T(2,128)(2,1)} %gain.1, ...), custom_call_target="tpu_custom_call" | custom-call | flops 17179869184 | bytes 16777216 | tf_op jit(solution)/shard_map/layer/pallas_call | solution.py:464
  255.9 2.4 store.1
